TPU v7x, 32 devices: a whole 2x2x4 slice. The times are simulated.
32 devices in a mesh: wide: 8 (over z, core), narrow: 4 (over y, x).
Axes of the slice: x: 2, y: 2, z: 4, core: 2. Of those that a mesh axis runs over, the one named last changes fastest.
Arguments:
- tridiag_vectors: float32 [128, 131072], P(('wide', 'narrow')), may hold values from -6 to 6
- reflectors: float32 [2, 131072, 256], P(None, 'wide'), may hold values from -0.015625 to 0.015625
- triangles: float32 [2, 256, 256], replicated, as said below
- lower_blocks: float32 [6, 1536, 1536], P(None, 'wide'), may hold values from -0.109375 to 0.109375
- diag_inverses: float32 [4, 1536, 1536], P(None, None, 'wide'), as said below
Outputs:
- transformed: float32 [128, 131072], P('narrow', 'wide')
- solved: float32 [128, 4, 1536], P('narrow', None, 'wide')
Inputs may be any that keep to these rules, and one draw needn't show every extreme that they name: `triangles`: zero below the diagonal, positive on it. `diag_inverses`: zero above the diagonal, positive on it.
All inputs are finite; a program needn't handle non-finite values.
Results may differ from a plain program's by a relative error of at most 0.00019.
Values sent between devices are 32-bit elements; how exact they have to be, the bound alone decides.
A program may use at most 128 MiB of HBM per device.

v0:
```python
import jax
import jax.numpy as jnp
from jax import lax
from jax.sharding import PartitionSpec as P

HIGHEST = lax.Precision.HIGHEST


def reflect(current, vectors, factor, products):
    coeffs = jnp.dot(products, factor.T, precision=HIGHEST)
    return current - jnp.dot(coeffs, vectors.T, precision=HIGHEST)


def add_piece(inverse, segment):
    return jnp.dot(segment, inverse, precision=HIGHEST)


def solve_chain(corner, lower_blocks, diag_inverses):
    local_count, panels, share_cols = corner.shape
    zeroed = jnp.zeros((local_count, share_cols), jnp.float32)
    pending = [zeroed] * panels
    results = [zeroed] * panels
    for source in reversed(range(panels)):
        remain = corner[:, source, :] - pending[source]
        solution = add_piece(
            diag_inverses[source], lax.all_gather(remain, "wide", axis=1, tiled=True)
        )
        results[source] = solution
        if source > 0:
            offset = source * (source - 1) // 2
            blocks = lower_blocks[offset : offset + source]
            partial_terms = jnp.einsum("ks,qsc->kqc", solution, blocks, precision=HIGHEST)
            scattered = lax.psum_scatter(partial_terms, "wide", scatter_dimension=2, tiled=True)
            for target in range(source):
                pending[target] = pending[target] + scattered[:, target, :]
    return jnp.stack(results, axis=1)


def body(tridiag_vectors, reflectors, triangles, lower_blocks, diag_inverses):
    wide_size = lax.axis_size("wide")
    spread = lax.all_to_all(
        tridiag_vectors, ("wide", "narrow"), split_axis=1, concat_axis=0, tiled=True
    )
    current = lax.all_to_all(spread, "narrow", split_axis=0, concat_axis=1, tiled=True)
    for which in (1, 0):
        products = lax.psum(jnp.dot(current, reflectors[which], precision=HIGHEST), "wide")
        current = reflect(current, reflectors[which], triangles[which], products)
    panels, panel_rows, share_cols = diag_inverses.shape
    corner_span = panels * panel_rows
    tail_cols = current[:, current.shape[1] - corner_span :]
    framed = tail_cols.reshape(tail_cols.shape[0], panels, wide_size, share_cols)
    received = lax.all_to_all(framed, "wide", split_axis=2, concat_axis=2, tiled=True)
    corner = received[:, :, wide_size - 1, :]
    solved = solve_chain(corner, lower_blocks, diag_inverses)
    return (current, solved)


def solution(mesh):
    placed = (
        P(("wide", "narrow"), None),
        P(None, "wide", None),
        P(),
        P(None, "wide", None),
        P(None, None, "wide"),
    )
    return jax.shard_map(
        body,
        mesh=mesh,
        in_specs=placed,
        out_specs=(P("narrow", "wide"), P("narrow", None, "wide")),
        check_vma=False,
    )
```

profile of v0, /device:TPU:0, one launch (start us, length us, event | category | flops | bytes accessed | tf_op | source)
XLA Modules:
  0.0 433.0 jit_solution(8765695923981802089)
XLA Ops:
  7.2 0.0 reduce-scatter.10.cloned.1.call-start
  7.2 56.5 %all_to_all.40 = f32[4,32,4096]{2,0,1:T(4,128)} all-to-all(f32[4,32,4096]{2,0,1:T(4,128)} %bitcast.93), channel_id=1, replica_groups=mesh['wide'=8,'narrow'=4] {'wide','narrow'}, dimensions={1} | all-to-all | bytes 4194304 | tf_op jit(solution)/shard_map/all_to_all | solution.py:41
  63.7 2.0 all_to_all.32
  65.6 28.2 %all_to_all.41 = f32[4,32,4096]{2,1,0:T(8,128)S(1)} all-to-all(f32[4,32,4096]{2,1,0:T(8,128)S(1)} %all_to_all.32), channel_id=1, replica_groups=mesh['wide'=8,'narrow'=4] {'narrow'}, dimensions={0} | all-to-all | bytes 4194304 | tf_op jit(solution)/shard_map/all_to_all | solution.py:44
  93.8 0.1 copy.39
  94.0 0.0 copy-start
  94.0 1.3 copy-done
  95.3 0.0 copy-start.2
  95.3 10.7 %fusion.4 = f32[32,256]{1,0:T(8,128)S(1)} fusion(f32[32,16384]{1,0:T(8,128)S(1)} %bitcast.83, f32[2,16384,256]{2,1,0:T(8,128)} %param.6), kind=kOutput, calls=%fused_computation.6 | convolution fusion | flops 1610612736 | bytes 18907136 | tf_op jit(solution)/shard_map/dot_general | solution.py:46
  106.0 26.1 %psum.14 = f32[32,256]{1,0:T(8,128)S(1)} all-reduce(f32[32,256]{1,0:T(8,128)S(1)} %fusion.4), channel_id=1, replica_groups=mesh['wide'=8,'narrow'=4] {'wide'}, use_global_device_ids=true, to_apply=%region_0.0 | all-reduce | flops 8192 | bytes 65536 | tf_op jit(solution)/shard_map/psum | solution.py:46
  132.1 0.0 copy-done.2
  132.1 0.3 fusion.33
  132.5 18.6 %convolution_subtract_fusion.1 = f32[32,16384]{1,0:T(8,128)S(1)} fusion(f32[32,16384]{1,0:T(8,128)} %bitcast.84, f32[32,256]{1,0:T(8,128)S(1)} %fusion.33, f32[2,16384,256]{2,1,0:T(8,128)} %param.6), kind=kOutput, calls=%fused_computation.1 | convolution fusion | flops 1611137024 | bytes 21004288 | tf_op jit(solution)/shard_map/dot_general | solution.py:11
  151.1 10.6 %fusion.1 = f32[32,256]{1,0:T(8,128)S(1)} fusion(f32[32,16384]{1,0:T(8,128)S(1)} %convolution_subtract_fusion.1, f32[2,16384,256]{2,1,0:T(8,128)} %param.6), kind=kOutput, calls=%fused_computation.3 | convolution fusion | flops 1610612736 | bytes 18907136 | tf_op jit(solution)/shard_map/dot_general | solution.py:46
  161.8 26.2 %psum.15 = f32[32,256]{1,0:T(8,128)S(1)} all-reduce(f32[32,256]{1,0:T(8,128)S(1)} %fusion.1), channel_id=1, replica_groups=mesh['wide'=8,'narrow'=4] {'wide'}, use_global_device_ids=true, to_apply=%region_1.0 | all-reduce | flops 8192 | bytes 65536 | tf_op jit(solution)/shard_map/psum | solution.py:46
  187.9 0.3 fusion.31
  188.3 17.3 %convolution_subtract_fusion = f32[32,16384]{1,0:T(8,128)S(1)} fusion(f32[32,16384]{1,0:T(8,128)S(1)} %convolution_subtract_fusion.1, f32[32,256]{1,0:T(8,128)S(1)} %fusion.31, f32[2,16384,256]{2,1,0:T(8,128)} %param.6), kind=kOutput, calls=%fused_computation | convolution fusion | flops 1611137024 | bytes 21004288 | tf_op jit(solution)/shard_map/dot_general | solution.py:11
  205.5 0.0 copy-start.1
  205.5 1.3 copy-done.1
  206.9 0.1 slice.90
  206.9 0.5 reshape.24
  207.4 0.6 copy.22
  208.0 29.0 %all_to_all.42 = f32[32,4,8,192]{3,0,1,2:T(8,128)S(1)} all-to-all(f32[32,4,8,192]{3,0,1,2:T(8,128)S(1)} %copy.22), channel_id=1, replica_groups=mesh['wide'=8,'narrow'=4] {'wide'}, dimensions={2} | all-to-all | bytes 1572864 | tf_op jit(solution)/shard_map/all_to_all | solution.py:52
  237.0 0.1 copy.23
  237.1 15.7 %all-gather = f32[32,1,1536]{0,1,2:T(1,128)S(1)} all-gather(f32[32,1,192]{0,1,2:T(1,128)S(1)} %copy.23), channel_id=2, replica_groups=mesh['wide'=8,'narrow'=4] {'wide'}, dimensions={2}, use_global_device_ids=true | all-gather | bytes 221184 | tf_op jit(solution)/shard_map/all_gather | solution.py:26
  252.9 2.6 fusion.21
  255.5 5.0 %fusion.10 = f32[32,3,1536]{2,0,1:T(8,128)} fusion(f32[6,192,1536]{2,1,0:T(8,128)} %param.8, f32[32,192]{1,0:T(8,128)S(1)} %fusion.21), kind=kOutput, calls=%fused_computation.12 | convolution fusion | flops 339738624 | bytes 4153344 | tf_op jit(solution)/shard_map/ks,qsc->kqc/dot_general | solution.py:32
  260.5 2.6 copy.28
  263.2 2.2 reshape.32
  265.4 0.0 reduce-scatter.10.cloned.1.call-update
  265.4 0.0 reduce-scatter.12.cloned.1.call-start
  265.5 29.5 %reduce-scatter.10.cloned.1.call-done = f32[192,96]{1,0:T(8,128)} async-done(((f32[1536,96]{1,0:T(8,128)}), f32[192,96]{1,0:T(8,128)}) %reduce-scatter.10.cloned.1.call-update) | async-done | bytes 73744
  295.0 1.1 reshape.33
  296.1 0.2 fusion.39
  296.3 0.1 copy.35
  296.4 0.1 copy.24
  296.5 16.0 %all-gather.1 = f32[32,1,1536]{0,1,2:T(1,128)S(1)} all-gather(f32[32,1,192]{0,1,2:T(1,128)S(1)} %copy.24), channel_id=3, replica_groups=mesh['wide'=8,'narrow'=4] {'wide'}, dimensions={2}, use_global_device_ids=true | all-gather | bytes 221184 | tf_op jit(solution)/shard_map/all_gather | solution.py:26
  312.5 2.6 fusion.19
  315.1 3.2 fusion.12
  318.3 0.8 copy.30
  319.1 1.8 reshape.34
  320.9 0.0 reduce-scatter.12.cloned.1.call-update
  320.9 0.0 reduce-scatter.14.cloned.1.call-start
  321.0 0.1 copy.37
  321.0 30.2 %reduce-scatter.12.cloned.1.call-done = f32[192,64]{1,0:T(8,128)} async-done(((f32[1536,64]{1,0:T(8,128)}), f32[192,64]{1,0:T(8,128)}) %reduce-scatter.12.cloned.1.call-update) | async-done | bytes 49168
  351.2 1.0 reshape.35
  352.3 0.2 fusion.40
  352.4 0.1 copy.38
  352.5 0.1 copy.25
  352.6 15.7 %all-gather.2 = f32[32,1,1536]{0,1,2:T(1,128)S(1)} all-gather(f32[32,1,192]{0,1,2:T(1,128)S(1)} %copy.25), channel_id=4, replica_groups=mesh['wide'=8,'narrow'=4] {'wide'}, dimensions={2}, use_global_device_ids=true | all-gather | bytes 221184 | tf_op jit(solution)/shard_map/all_gather | solution.py:26
  368.4 2.6 fusion.17
  371.0 4.8 %convolution_bitcast_fusion = f32[1536,32]{1,0:T(8,128)} fusion(f32[32,192]{1,0:T(8,128)S(1)} %fusion.17, f32[6,192,1536]{2,1,0:T(8,128)} %param.8), kind=kOutput, calls=%fused_computation.14 | convolution fusion | flops 113246208 | bytes 1400832 | tf_op jit(solution)/shard_map/ks,qsc->kqc/dot_general | solution.py:32
  375.8 0.0 reduce-scatter.14.cloned.1.call-update
  375.8 0.1 copy.34
  375.9 0.1 copy.36
  375.9 30.3 %reduce-scatter.14.cloned.1.call-done = f32[192,32]{1,0:T(8,128)} async-done(((f32[1536,32]{1,0:T(8,128)}), f32[192,32]{1,0:T(8,128)}) %reduce-scatter.14.cloned.1.call-update) | async-done | bytes 24592
  406.3 1.0 copy.33
  407.2 0.1 copy.26
  407.3 15.7 %all-gather.3 = f32[32,1,1536]{0,1,2:T(1,128)S(1)} all-gather(f32[32,1,192]{0,1,2:T(1,128)S(1)} %copy.26), channel_id=5, replica_groups=mesh['wide'=8,'narrow'=4] {'wide'}, dimensions={2}, use_global_device_ids=true | all-gather | bytes 221184 | tf_op jit(solution)/shard_map/all_gather | solution.py:26
  423.1 2.6 fusion.28
  425.7 0.7 copy.27
  (6 shorter events, 0.1 us)
Async XLA Ops:
  7.2 287.9 %reduce-scatter.10.cloned.1.call-start = ((), (), s32[]{:S(2)}) async-start(), calls=%async_computation.6 | async-start | bytes 884736
  94.0 1.3 copy-start
  95.3 36.8 %copy-start.2 = (f32[2,256,256]{2,1,0:T(8,128)S(1)}, f32[2,256,256]{2,1,0:T(8,128)}, u32[]{:S(2)}) copy-start(f32[2,256,256]{2,1,0:T(8,128)} %param.7) | copy-start | bytes 1572868
  205.5 1.3 copy-start.1
  265.4 85.8 %reduce-scatter.12.cloned.1.call-start = ((), (), s32[]{:S(2)}) async-start(), calls=%async_computation.7 | async-start | bytes 884736
  320.9 85.4 %reduce-scatter.14.cloned.1.call-start = ((), (), s32[]{:S(2)}) async-start(), calls=%async_computation.8 | async-start | bytes 884736
Sparse Core Ops, SparseCore 0:
  265.6 29.4 reduce-scatter.9
  321.0 30.1 reduce-scatter.11
  375.9 30.2 reduce-scatter.13
where the time goes:
time: 434 us; the launch traced here: 433 us
  blocking collectives  229 us (53%)
  waiting for transfers between devices  90.1 us (21%)
  matrix products  81.5 us (19%)
  local copies, waits for them, and re-layouts  18.2 us (4%)
  between operations  14 us (3%)
    unnamed x6, waiting for transfers between devices  90.1 us
    all_gather x4, blocking collectives, solve_chain(): lax.all_gather(remain, 'wide', axis=1, tiled=True)  63.2 us
    all_to_all x1, blocking collectives, body(): lax.all_to_all(tridiag_vectors, ('wide', 'narrow'), split_axis=1, concat_...  56.5 us
    psum x2, blocking collectives, body(): lax.psum(jnp.dot(current, reflectors[which], precision=HIGHEST), 'wide')  52.3 us
    dot_general x2, matrix products, reflect(): return current - jnp.dot(coeffs, vectors.T, precision=HIGHEST)  35.9 us
    all_to_all x1, blocking collectives, body(): lax.all_to_all(framed, 'wide', split_axis=2, concat_axis=2, tiled=True)  29 us
    all_to_all x1, blocking collectives, body(): lax.all_to_all(spread, 'narrow', split_axis=0, concat_axis=1, tiled=True)  28.2 us
    dot_general x2, matrix products, body(): jnp.dot(current, reflectors[which], precision=HIGHEST)  21.3 us
  transfers between devices with their start and end apart: 3, of which 3 were waited for; matrix products, arithmetic and copies ran while one was open for 0% of the time, Pallas kernels for 0%

commit v1 on v0

--- a/solution.py
+++ b/solution.py
@@ -22,9 +22,18 @@
     results = [zeroed] * panels
     for source in reversed(range(panels)):
         remain = corner[:, source, :] - pending[source]
-        solution = add_piece(
-            diag_inverses[source], lax.all_gather(remain, "wide", axis=1, tiled=True)
-        )
+
+        def reach_ports_in(state, at_axis):
+            block_now = lax.all_to_all(
+                jnp.stack(lax.psum(1, axis_name="wide") * [state], axis=0),
+                concat_axis=0,
+                split_axis=0,
+                axis_name="wide",
+            )
+            left_arr = jnp.concatenate(block_now, axis=at_axis)
+            return left_arr
+
+        solution = add_piece(diag_inverses[source], reach_ports_in(remain, 1))
         results[source] = solution
         if source > 0:
             offset = source * (source - 1) // 2

time: 434 us -> 420 us (0.968)
  blocking collectives: 229 us -> 214 us
    all_gather x4 -> x0, blocking collectives: 63.2 us -> none  [solve_chain(): lax.all_gather(remain, 'wide', axis=1, tiled=True)]
    all_to_all x0 -> x4, blocking collectives: none -> 48.5 us  [reach_ports_in(): lax.all_to_all(jnp.stack(lax.psum(1, axis_name='wide') * [state], axis=0)...]
where the time goes in v1:
time: 420 us
  blocking collectives  214 us (51%)
  waiting for transfers between devices  91.3 us (22%)
  matrix products  80.7 us (19%)
  local copies, waits for them, and re-layouts  19 us (5%)
  between operations  14 us (3%)
    unnamed x6, waiting for transfers between devices  91.3 us
    all_to_all x1, blocking collectives, body(): lax.all_to_all(tridiag_vectors, ('wide', 'narrow'), split_axis=1, concat_...  56.5 us
    psum x2, blocking collectives, body(): lax.psum(jnp.dot(current, reflectors[which], precision=HIGHEST), 'wide')  52.3 us
    all_to_all x4, blocking collectives, reach_ports_in(): lax.all_to_all(jnp.stack(lax.psum(1, axis_name='wide') * [state], axis=0)...  48.5 us
    dot_general x2, matrix products, reflect(): return current - jnp.dot(coeffs, vectors.T, precision=HIGHEST)  35.9 us
    all_to_all x1, blocking collectives, body(): lax.all_to_all(framed, 'wide', split_axis=2, concat_axis=2, tiled=True)  29 us
    all_to_all x1, blocking collectives, body(): lax.all_to_all(spread, 'narrow', split_axis=0, concat_axis=1, tiled=True)  28.2 us
    dot_general x2, matrix products, body(): jnp.dot(current, reflectors[which], precision=HIGHEST)  21.3 us
  transfers between devices with their start and end apart: 3, of which 3 were waited for; matrix products, arithmetic and copies ran while one was open for 0% of the time, Pallas kernels for 0%

profile of v1, /device:TPU:0, one launch (start us, length us, event | category | flops | bytes accessed | tf_op | source)
XLA Modules:
  0.0 419.6 jit_solution(17973680428649461891)
XLA Ops:
  7.2 0.0 reduce-scatter.10.cloned.1.call-start
  7.2 56.5 %all_to_all.60 = f32[4,32,4096]{2,0,1:T(4,128)} all-to-all(f32[4,32,4096]{2,0,1:T(4,128)} %bitcast.97), channel_id=1, replica_groups=mesh['wide'=8,'narrow'=4] {'wide','narrow'}, dimensions={1} | all-to-all | bytes 4194304 | tf_op jit(solution)/shard_map/all_to_all | solution.py:50
  63.7 2.0 all_to_all.44
  65.6 28.2 %all_to_all.61 = f32[4,32,4096]{2,1,0:T(8,128)S(1)} all-to-all(f32[4,32,4096]{2,1,0:T(8,128)S(1)} %all_to_all.44), channel_id=1, replica_groups=mesh['wide'=8,'narrow'=4] {'narrow'}, dimensions={0} | all-to-all | bytes 4194304 | tf_op jit(solution)/shard_map/all_to_all | solution.py:53
  93.8 0.1 copy.32
  94.0 0.0 copy-start
  94.0 1.3 copy-done
  95.3 10.7 %fusion.4 = f32[32,256]{1,0:T(8,128)S(1)} fusion(f32[32,16384]{1,0:T(8,128)S(1)} %bitcast.91, f32[2,16384,256]{2,1,0:T(8,128)} %param.6), kind=kOutput, calls=%fused_computation.6 | convolution fusion | flops 1610612736 | bytes 18907136 | tf_op jit(solution)/shard_map/dot_general | solution.py:55
  106.0 26.1 %psum.14 = f32[32,256]{1,0:T(8,128)S(1)} all-reduce(f32[32,256]{1,0:T(8,128)S(1)} %fusion.4), channel_id=1, replica_groups=mesh['wide'=8,'narrow'=4] {'wide'}, use_global_device_ids=true, to_apply=%region_0.0 | all-reduce | flops 8192 | bytes 65536 | tf_op jit(solution)/shard_map/psum | solution.py:55
  132.1 0.0 copy-done.2
  132.1 0.3 fusion.33
  132.5 18.6 %convolution_subtract_fusion.1 = f32[32,16384]{1,0:T(8,128)S(1)} fusion(f32[32,16384]{1,0:T(8,128)} %bitcast.92, f32[32,256]{1,0:T(8,128)S(1)} %fusion.33, f32[2,16384,256]{2,1,0:T(8,128)} %param.6), kind=kOutput, calls=%fused_computation.1 | convolution fusion | flops 1611137024 | bytes 21004288 | tf_op jit(solution)/shard_map/dot_general | solution.py:11
  151.1 10.6 %fusion.1 = f32[32,256]{1,0:T(8,128)S(1)} fusion(f32[32,16384]{1,0:T(8,128)S(1)} %convolution_subtract_fusion.1, f32[2,16384,256]{2,1,0:T(8,128)} %param.6), kind=kOutput, calls=%fused_computation.3 | convolution fusion | flops 1610612736 | bytes 18907136 | tf_op jit(solution)/shard_map/dot_general | solution.py:55
  161.8 26.2 %psum.15 = f32[32,256]{1,0:T(8,128)S(1)} all-reduce(f32[32,256]{1,0:T(8,128)S(1)} %fusion.1), channel_id=1, replica_groups=mesh['wide'=8,'narrow'=4] {'wide'}, use_global_device_ids=true, to_apply=%region_1.0 | all-reduce | flops 8192 | bytes 65536 | tf_op jit(solution)/shard_map/psum | solution.py:55
  187.9 0.3 fusion.31
  188.3 17.3 %convolution_subtract_fusion = f32[32,16384]{1,0:T(8,128)S(1)} fusion(f32[32,16384]{1,0:T(8,128)S(1)} %convolution_subtract_fusion.1, f32[32,256]{1,0:T(8,128)S(1)} %fusion.31, f32[2,16384,256]{2,1,0:T(8,128)} %param.6), kind=kOutput, calls=%fused_computation | convolution fusion | flops 1611137024 | bytes 21004288 | tf_op jit(solution)/shard_map/dot_general | solution.py:11
  205.5 0.0 copy-start.1
  205.5 1.3 copy-done.1
  206.9 0.1 slice.90
  206.9 0.5 reshape.71
  207.4 0.6 copy.15
  208.0 29.0 %all_to_all.62 = f32[32,4,8,192]{3,0,1,2:T(8,128)S(1)} all-to-all(f32[32,4,8,192]{3,0,1,2:T(8,128)S(1)} %copy.15), channel_id=1, replica_groups=mesh['wide'=8,'narrow'=4] {'wide'}, dimensions={2} | all-to-all | bytes 1572864 | tf_op jit(solution)/shard_map/all_to_all | solution.py:61
  237.0 12.1 %all_to_all.63 = f32[8,32,192]{2,1,0:T(8,128)S(1)} all-to-all(f32[8,32,192]{2,1,0:T(8,128)S(1)} %stack.18), channel_id=1, replica_groups=mesh['wide'=8,'narrow'=4] {'wide'}, dimensions={0} | all-to-all | bytes 393216 | tf_op jit(solution)/shard_map/all_to_all | solution.py:27
  249.2 0.2 copy.16
  249.3 0.1 reshape.73
  249.4 2.5 fusion.21
  251.9 5.0 %fusion.10 = f32[32,3,1536]{2,0,1:T(8,128)} fusion(f32[6,192,1536]{2,1,0:T(8,128)} %param.8, f32[32,192]{1,0:T(8,128)S(1)} %fusion.21), kind=kOutput, calls=%fused_computation.12 | convolution fusion | flops 339738624 | bytes 4153344 | tf_op jit(solution)/shard_map/ks,qsc->kqc/dot_general | solution.py:41
  257.0 2.6 copy.21
  259.6 2.2 reshape.83
  261.8 0.0 reduce-scatter.10.cloned.1.call-update
  261.8 0.0 reduce-scatter.12.cloned.1.call-start
  261.9 29.6 %reduce-scatter.10.cloned.1.call-done = f32[192,96]{1,0:T(8,128)} async-done(((f32[1536,96]{1,0:T(8,128)}), f32[192,96]{1,0:T(8,128)}) %reduce-scatter.10.cloned.1.call-update) | async-done | bytes 73744
  291.4 1.1 reshape.84
  292.5 0.2 fusion.42
  292.7 0.1 copy.28
  292.9 12.1 %all_to_all.64 = f32[8,32,192]{2,1,0:T(8,128)S(1)} all-to-all(f32[8,32,192]{2,1,0:T(8,128)S(1)} %stack.19), channel_id=1, replica_groups=mesh['wide'=8,'narrow'=4] {'wide'}, dimensions={0} | all-to-all | bytes 393216 | tf_op jit(solution)/shard_map/all_to_all | solution.py:27
  305.0 0.2 copy.17
  305.1 0.1 reshape.75
  305.3 2.5 fusion.19
  307.7 3.2 fusion.12
  310.9 0.8 copy.23
  311.7 1.8 reshape.85
  313.5 0.0 reduce-scatter.12.cloned.1.call-update
  313.5 0.0 reduce-scatter.14.cloned.1.call-start
  313.5 0.1 copy.30
  313.6 30.8 %reduce-scatter.12.cloned.1.call-done = f32[192,64]{1,0:T(8,128)} async-done(((f32[1536,64]{1,0:T(8,128)}), f32[192,64]{1,0:T(8,128)}) %reduce-scatter.12.cloned.1.call-update) | async-done | bytes 49168
  344.4 1.0 reshape.86
  345.5 0.2 fusion.43
  345.6 0.1 copy.31
  345.7 12.1 %all_to_all.65 = f32[8,32,192]{2,1,0:T(8,128)S(1)} all-to-all(f32[8,32,192]{2,1,0:T(8,128)S(1)} %stack.20), channel_id=1, replica_groups=mesh['wide'=8,'narrow'=4] {'wide'}, dimensions={0} | all-to-all | bytes 393216 | tf_op jit(solution)/shard_map/all_to_all | solution.py:27
  357.9 0.2 copy.18
  358.0 0.1 reshape.77
  358.1 2.5 fusion.17
  360.6 4.8 %convolution_bitcast_fusion = f32[1536,32]{1,0:T(8,128)} fusion(f32[32,192]{1,0:T(8,128)S(1)} %fusion.17, f32[6,192,1536]{2,1,0:T(8,128)} %param.8), kind=kOutput, calls=%fused_computation.14 | convolution fusion | flops 113246208 | bytes 1400832 | tf_op jit(solution)/shard_map/ks,qsc->kqc/dot_general | solution.py:41
  365.4 0.0 reduce-scatter.14.cloned.1.call-update
  365.4 0.1 copy.27
  365.5 0.1 copy.29
  365.5 30.9 %reduce-scatter.14.cloned.1.call-done = f32[192,32]{1,0:T(8,128)} async-done(((f32[1536,32]{1,0:T(8,128)}), f32[192,32]{1,0:T(8,128)}) %reduce-scatter.14.cloned.1.call-update) | async-done | bytes 24592
  396.4 1.0 copy.26
  397.4 12.1 %all_to_all.66 = f32[8,32,192]{2,1,0:T(8,128)S(1)} all-to-all(f32[8,32,192]{2,1,0:T(8,128)S(1)} %stack.21), channel_id=1, replica_groups=mesh['wide'=8,'narrow'=4] {'wide'}, dimensions={0} | all-to-all | bytes 393216 | tf_op jit(solution)/shard_map/all_to_all | solution.py:27
  409.5 0.2 copy.19
  409.7 0.1 reshape.80
  409.8 2.4 fusion.28
  412.3 0.7 copy.20
  (11 shorter events, 0.2 us)
Async XLA Ops:
  7.2 284.3 %reduce-scatter.10.cloned.1.call-start = ((), (), s32[]{:S(2)}) async-start(), calls=%async_computation.10 | async-start | bytes 884736
  94.0 1.3 copy-start
  95.3 36.8 %copy-start.2 = (f32[2,256,256]{2,1,0:T(8,128)S(1)}, f32[2,256,256]{2,1,0:T(8,128)}, u32[]{:S(2)}) copy-start(f32[2,256,256]{2,1,0:T(8,128)} %param.7) | copy-start | bytes 1572868
  205.5 1.3 copy-start.1
  261.8 82.6 %reduce-scatter.12.cloned.1.call-start = ((), (), s32[]{:S(2)}) async-start(), calls=%async_computation.11 | async-start | bytes 884736
  313.5 82.9 %reduce-scatter.14.cloned.1.call-start = ((), (), s32[]{:S(2)}) async-start(), calls=%async_computation.12 | async-start | bytes 884736
Sparse Core Ops, SparseCore 0:
  262.0 29.4 reduce-scatter.9
  313.6 30.7 reduce-scatter.11
  365.5 30.8 reduce-scatter.13
